TPU v7x, 512 devices: a whole 4x8x8 slice. The times are simulated.
512 devices in a mesh: seq: 32 (over y, z_hi), section: 4 (over x), tp: 4 (over z_lo, core).
Axes of the slice: x: 4, y: 8, z: 8 (z_hi: 4, z_lo: 2; z = z_hi * 2 + z_lo), core: 2. Of those that a mesh axis runs over, the one named last changes fastest.
Arguments:
- token_ids: int32 [2048], P('seq'), may hold values from 0 to 65535
- embed_columns: bfloat16 [4096, 65536], P(('tp', 'seq')), may hold values from -6 to 6
- norm_gain: bfloat16 [4, 4096], P('section'), may hold values from 0.099609375 to 1.8984375
- qkv_weight: bfloat16 [4, 4096, 4096], P('section', 'seq', 'tp'), may hold values from -1 to 1
- out_weight: bfloat16 [4, 4096, 2048], P('section', 'seq', 'tp'), may hold values from -0.125 to 0.125
Outputs:
- layer_states: bfloat16 [4, 2048, 4096], P('section', 'seq', 'tp')
All inputs are finite; a program needn't handle non-finite values.
Results may differ from a plain program's by a relative error of at most 0.02.
Values may be sent and summed in bfloat16 or wider, within the bound.
A program may use at most 128 MiB of HBM per device.

v0:
```python
import jax
import jax.numpy as jnp
from jax import lax
from jax.sharding import PartitionSpec as P

QUERY_HEADS = 16
KEY_VALUE_HEADS = 8
HEAD_WIDTH = 128


EPS = 1e-05
ROPE_BASE = 500000.0
MASKED = -1e30


def in_order(blocks, dim):
    shape = list(blocks.shape[1:])
    shape[dim] *= blocks.shape[0]
    return jnp.moveaxis(blocks, 0, dim).reshape(shape)


def sent_to_all(value, axis):
    copies = jnp.broadcast_to(value, (lax.axis_size(axis), *value.shape))
    return lax.all_to_all(copies, axis, split_axis=0, concat_axis=0, tiled=True)


def gathered_copies(value, axis, dim):
    return in_order(sent_to_all(value, axis), dim)


def in_blocks(value, dim, length):
    before, after = (value.shape[:dim], value.shape[dim + 1 :])
    return jnp.moveaxis(value.reshape(*before, length, -1, *after), dim, 0)


def sum_at_owner(value, axis, dim):
    length = lax.axis_size(axis)
    blocks = lax.all_to_all(in_blocks(value, dim, length), axis, 0, 0, tiled=True)
    return jnp.sum(blocks.astype(jnp.float32), axis=0)


def passed_along(value, axis, steps):
    count = lax.axis_size(axis)
    leading, last = (max(0, -steps), min(count, count - steps))
    return lax.ppermute(value, axis, [(source, source + steps) for source in range(leading, last)])


def sent_together(arrays, axis, dim, along):
    ends, at = ([], 0)
    for a in arrays[:-1]:
        at += a.shape[along]
        ends.append(at)
    both = jnp.concatenate(arrays, axis=along)
    return tuple(jnp.split(lax.all_gather(both, axis, axis=dim, tiled=True), ends, axis=along))


def rope_tables(positions, head_size):
    half_width = head_size // 2
    inverse_freq = ROPE_BASE ** (-jnp.arange(half_width).astype(jnp.float32) * (2.0 / head_size))
    angles = positions.astype(jnp.float32)[:, None] * inverse_freq[None, :]
    return (jnp.cos(angles), jnp.sin(angles))


def rotate_half(heads, cosine_table, sine_values):
    half_width = heads.shape[-1] // 2
    first_half = heads[..., :half_width]
    second = heads[..., half_width:]
    cosine_table = cosine_table[:, None, :]
    sine_values = sine_values[:, None, :]
    return jnp.concatenate(
        [
            first_half * cosine_table - second * sine_values,
            second * cosine_table + first_half * sine_values,
        ],
        axis=-1,
    )


def norm_rows(row_block, gain_row):
    values = row_block.astype(jnp.float32)
    inverse_rms = lax.rsqrt(jnp.mean(values * values, axis=-1, keepdims=True) + EPS)
    return (values * inverse_rms * gain_row[None, :]).astype(jnp.bfloat16)


def widen(current):
    return gathered_copies(current, "tp", 1)


def project(full_rows, gain_row, qkv_full, positions, query_heads, key_value_heads):
    row_count = full_rows.shape[0]
    normed = norm_rows(full_rows, gain_row)
    projected_rows = jnp.dot(normed, qkv_full, preferred_element_type=jnp.float32)
    projected_rows = projected_rows.reshape(
        row_count, query_heads + 2 * key_value_heads, HEAD_WIDTH
    )
    cosine_table, sine_values = rope_tables(positions, HEAD_WIDTH)
    query_rows = rotate_half(projected_rows[:, :query_heads], cosine_table, sine_values).astype(
        jnp.bfloat16
    )
    key_head_rows = rotate_half(
        projected_rows[:, query_heads : query_heads + key_value_heads], cosine_table, sine_values
    ).astype(jnp.bfloat16)
    value_head_rows = projected_rows[:, query_heads + key_value_heads :].astype(jnp.bfloat16)
    return (query_rows, key_head_rows, value_head_rows)


def attend(query_rows, key_head_rows, value_head_rows, allowed):
    row_count, query_heads, head_size = query_rows.shape
    key_value_heads = key_head_rows.shape[1]
    query_groups = query_rows.reshape(
        row_count, key_value_heads, query_heads // key_value_heads, head_size
    )
    scores = jnp.einsum(
        "rkph,ckh->kprc", query_groups, key_head_rows, preferred_element_type=jnp.float32
    ) * head_size ** (-0.5)
    scores = jnp.where(allowed[None, None], scores, MASKED)
    weights = jax.nn.softmax(scores, axis=-1).astype(jnp.bfloat16)
    attended = jnp.einsum(
        "kprc,ckh->rkph", weights, value_head_rows, preferred_element_type=jnp.float32
    )
    return attended.reshape(row_count, query_heads * head_size).astype(jnp.bfloat16)


def combine(current, attended, out_full):
    partial_value = lax.dot_general(
        attended, out_full, (((1,), (1,)), ((), ())), preferred_element_type=jnp.float32
    )
    summed = sum_at_owner(partial_value.astype(jnp.bfloat16), "tp", 1)
    return (current.astype(jnp.float32) + summed).astype(jnp.bfloat16)


def advance(new_rows):
    return passed_along(new_rows, "section", 1)


def body(token_ids, embed_columns, norm_gain, qkv_weight, out_weight):
    seq_count = lax.axis_size("seq")
    section_count = lax.axis_size("section")
    tensor_parallel_count = lax.axis_size("tp")
    group_index = lax.axis_index("seq")
    section_index = lax.axis_index("section")
    block_row_slice = token_ids.shape[0]
    feature_slice = embed_columns.shape[0]
    feature_cols = feature_slice * seq_count
    query_heads = QUERY_HEADS // tensor_parallel_count
    key_value_heads = KEY_VALUE_HEADS // tensor_parallel_count
    every_id = gathered_copies(token_ids, "seq", 0)
    looked = jnp.take(embed_columns, every_id, axis=1)
    by_block = looked.reshape(feature_slice, seq_count, block_row_slice)
    anchor_part = jnp.broadcast_to(by_block[:, :1], by_block.shape)
    outgoing = jnp.concatenate([anchor_part, by_block], axis=2).reshape(
        feature_slice, seq_count * 2 * block_row_slice
    )
    arrived = lax.all_to_all(outgoing, "seq", split_axis=1, concat_axis=0, tiled=True)
    residual = arrived.T
    qkv_full, out_full = sent_together((qkv_weight, out_weight), "seq", 1, 2)
    qkv_full = qkv_full[0]
    out_full = out_full[0]
    gain_row = norm_gain[0].astype(jnp.float32)
    outputs = jnp.zeros((block_row_slice, feature_cols), jnp.bfloat16)
    half_rows = block_row_slice // 2
    slot_count = 4
    step_total = slot_count + section_count - 1
    key_cache = jnp.zeros((2 * block_row_slice, key_value_heads, HEAD_WIDTH), jnp.bfloat16)
    value_cache = jnp.zeros((2 * block_row_slice, key_value_heads, HEAD_WIDTH), jnp.bfloat16)
    received = jnp.zeros((half_rows, residual.shape[1]), jnp.bfloat16)
    column = jnp.arange(2 * block_row_slice)[None, :]
    for step_number in range(step_total):
        offset = step_number - section_index
        is_live = (offset >= 0) & (offset < slot_count)
        slot_index = jnp.clip(offset, 0, slot_count - 1)
        row_start = slot_index * half_rows
        embedded_part = lax.dynamic_slice_in_dim(residual, row_start, half_rows, 0)
        current = jnp.where(section_index == 0, embedded_part, received)
        combined = row_start + jnp.arange(half_rows)
        positions = jnp.where(
            combined < block_row_slice,
            combined,
            group_index * block_row_slice + combined - block_row_slice,
        )
        query_rows, key_head_rows, value_head_rows = project(
            widen(current), gain_row, qkv_full, positions, query_heads, key_value_heads
        )
        key_cache = lax.dynamic_update_slice_in_dim(key_cache, key_head_rows, row_start, 0)
        value_cache = lax.dynamic_update_slice_in_dim(value_cache, value_head_rows, row_start, 0)
        row_ids = combined[:, None]
        allowed = (column <= row_ids) & (
            (column >= block_row_slice) | (row_ids < block_row_slice) | (group_index > 0)
        )
        attended = attend(query_rows, key_cache, value_cache, allowed)
        new_rows = combine(current, attended, out_full)
        placed = lax.dynamic_update_slice_in_dim(
            outputs, new_rows, jnp.maximum(row_start - block_row_slice, 0), 0
        )
        outputs = jnp.where(is_live & (slot_index >= 2), placed, outputs)
        if step_number + 1 < step_total:
            received = advance(new_rows)
    return outputs[None]


def solution(mesh):
    placed = (
        P("seq"),
        P(("tp", "seq"), None),
        P("section", None),
        P("section", "seq", "tp"),
        P("section", "seq", "tp"),
    )
    return jax.shard_map(
        body, mesh=mesh, in_specs=placed, out_specs=P("section", "seq", "tp"), check_vma=False
    )
```

profile of v0, /device:TPU:1, one launch (start us, length us, event | category | flops | bytes accessed | tf_op | source)
XLA Modules:
  0.0 463.0 jit_solution(14935412570439493748)
XLA Ops:
  6.5 1.8 pad_maximum_fusion
  8.4 1.3 broadcast_in_dim.89
  9.7 16.5 %all-to-all-start = ((s32[32,1,64]{2,1,0:T(1,128)}), s32[32,1,64]{2,1,0:T(1,128)S(1)}, u32[]{:S(2)}, u32[]{:S(2)}) async-start(s32[32,1,64]{2,1,0:T(1,128)} %broadcast_in_dim.89), calls=%async_computation | async-start | bytes 32768 | tf_op jit(solution)/shard_map/all_to_all | solution.py:24
  26.3 13.7 %copy.58 = bf16[32,65536]{0,1:T(8,128)(2,1)} copy(bf16[32,65536]{1,0:T(8,128)(2,1)} %param.6) | data formatting | bytes 8388608 | tf_op args[1]
  41.3 13.6 %gather_fusion = bf16[2048,32]{1,0:T(8,128)(2,1)S(1)} fusion(bf16[32,65536]{0,1:T(8,128)(2,1)} %copy.58, s32[2048]{0:T(1024)S(1)} %broadcast_clamp_fusion), kind=kCustom, calls=%fused_computation | custom fusion | bytes 270336 | tf_op jit(solution)/shard_map/jit(_take)/gather | solution.py:148
  55.3 0.8 pad_maximum_fusion.1
  56.1 11.7 %all-to-all-start.1 = ((bf16[32,32,128]{2,0,1:T(8,128)(2,1)}), bf16[32,32,128]{2,0,1:T(8,128)(2,1)S(1)}, u32[]{:S(2)}, u32[]{:S(2)}) async-start(bf16[32,32,128]{2,0,1:T(8,128)(2,1)} %pad_maximum_fusion.1), calls=%async_computation.1 | async-start | bytes 524288 | tf_op jit(solution)/shard_map/all_to_all | solution.py:154
  68.0 11.5 %all-to-all-done.1 = bf16[32,32,128]{2,0,1:T(8,128)(2,1)S(1)} async-done(((bf16[32,32,128]{2,0,1:T(8,128)(2,1)}), bf16[32,32,128]{2,0,1:T(8,128)(2,1)S(1)}, u32[]{:S(2)}, u32[]{:S(2)}) %all-to-all-start.1) | async-done | bytes 262176 | tf_op jit(solution)/shard_map/all_to_all | solution.py:154
  80.9 6.7 %all-to-all-start.2 = ((bf16[4,32,1024]{2,1,0:T(8,128)(2,1)}), bf16[4,32,1024]{2,1,0:T(8,128)(2,1)S(1)}, u32[]{:S(2)}, u32[]{:S(2)}) async-start(bf16[4,32,1024]{2,1,0:T(8,128)(2,1)} %broadcast_in_dim.95), calls=%async_computation.2 | async-start | bytes 524288 | tf_op jit(solution)/shard_map/all_to_all | solution.py:24
  88.2 33.4 %all-to-all-done.2 = bf16[4,32,1024]{2,1,0:T(8,128)(2,1)S(1)} async-done(((bf16[4,32,1024]{2,1,0:T(8,128)(2,1)}), bf16[4,32,1024]{2,1,0:T(8,128)(2,1)S(1)}, u32[]{:S(2)}, u32[]{:S(2)}) %all-to-all-start.2) | async-done | bytes 262176 | tf_op jit(solution)/shard_map/all_to_all | solution.py:24
  122.2 76.9 %all-gather.2.cloned.1.call-done = bf16[1,4096,1536]{2,1,0:T(8,128)(2,1)} async-done(((bf16[1,128,1536]{2,1,0:T(8,128)(2,1)}), bf16[1,4096,1536]{2,1,0:T(8,128)(2,1)}) %all-gather.2.cloned.1.call-update) | async-done | bytes 12582928 | tf_op jit(solution)/shard_map/all_gather | solution.py:54
  199.1 7.6 %slice_bitcast_fusion = bf16[1024,4096]{0,1:T(8,128)(2,1)} fusion(bf16[1,4096,1536]{2,1,0:T(8,128)(2,1)} %all-gather.2.cloned.1.call-done), kind=kLoop, calls=%fused_computation.8 | loop fusion | bytes 16777216 | tf_op jit(solution)/shard_map/dot_general | solution.py:92
  206.7 11.3 %copy.62 = bf16[1024,4096]{1,0:T(8,128)(2,1)} copy(bf16[1024,4096]{0,1:T(8,128)(2,1)} %slice_bitcast_fusion) | data formatting | bytes 16777216 | tf_op jit(solution)/shard_map/dot_general | solution.py:92
  217.9 5.9 %fusion.149 = f32[32,8,128]{2,0,1:T(8,128)S(1)} fusion(bf16[32,4096,1]{1,0,2:T(8,128)(2,1)S(1)} %reshape.1091, bf16[8,128,4096]{2,1,0:T(8,128)(2,1)} %bitcast.267), kind=kOutput, calls=%fused_computation.337 | convolution fusion | flops 268435456 | bytes 8781824 | tf_op jit(solution)/shard_map/dot_general | solution.py:92
  225.0 3.5 convolution_convert_fusion.6
  228.5 0.7 copy.144
  229.2 5.1 %all-to-all-start.3 = ((bf16[4,32,1024]{2,1,0:T(8,128)(2,1)}), bf16[4,32,1024]{2,1,0:T(8,128)(2,1)S(1)}, u32[]{:S(2)}, u32[]{:S(2)}) async-start(bf16[4,32,1024]{2,1,0:T(8,128)(2,1)} %bitcast.266), calls=%async_computation.3 | async-start | bytes 524288 | tf_op jit(solution)/shard_map/all_to_all | solution.py:38
  234.3 4.9 %all-to-all-done.3 = bf16[4,32,1024]{2,1,0:T(8,128)(2,1)S(1)} async-done(((bf16[4,32,1024]{2,1,0:T(8,128)(2,1)}), bf16[4,32,1024]{2,1,0:T(8,128)(2,1)S(1)}, u32[]{:S(2)}, u32[]{:S(2)}) %all-to-all-start.3) | async-done | bytes 262176 | tf_op jit(solution)/shard_map/all_to_all | solution.py:38
  239.3 3.1 collective-permute-start
  242.5 1.2 collective-permute-done
  243.7 9.3 %all_to_all.92 = bf16[4,32,1024]{2,1,0:T(8,128)(2,1)S(1)} all-to-all(bf16[4,32,1024]{2,1,0:T(8,128)(2,1)S(1)} %broadcast_in_dim.99), channel_id=1, replica_groups=mesh['seq'=32,'section'=4,'tp'=4] {'tp'}, dimensions={0} | all-to-all | bytes 524288 | tf_op jit(solution)/shard_map/all_to_all | solution.py:24
  253.7 6.0 %fusion.150 = f32[32,8,128]{2,0,1:T(8,128)S(1)} fusion(bf16[32,4096,1]{1,0,2:T(8,128)(2,1)S(1)} %reshape.1094, bf16[8,128,4096]{2,1,0:T(8,128)(2,1)} %bitcast.268), kind=kOutput, calls=%fused_computation.338 | convolution fusion | flops 268435456 | bytes 8781824 | tf_op jit(solution)/shard_map/dot_general | solution.py:92
  260.7 3.5 convolution_convert_fusion.5
  264.2 0.7 copy.143
  264.9 4.4 all-to-all-start.5
  270.0 4.4 all-to-all-done.5
  274.5 4.0 collective-permute-start.1
  278.6 1.2 collective-permute-done.1
  279.8 9.2 %all_to_all.93 = bf16[4,32,1024]{2,1,0:T(8,128)(2,1)S(1)} all-to-all(bf16[4,32,1024]{2,1,0:T(8,128)(2,1)S(1)} %broadcast_in_dim.101), channel_id=1, replica_groups=mesh['seq'=32,'section'=4,'tp'=4] {'tp'}, dimensions={0} | all-to-all | bytes 524288 | tf_op jit(solution)/shard_map/all_to_all | solution.py:24
  289.7 6.0 %fusion.151 = f32[32,8,128]{2,0,1:T(8,128)S(1)} fusion(bf16[32,4096,1]{1,0,2:T(8,128)(2,1)S(1)} %reshape.1097, bf16[8,128,4096]{2,1,0:T(8,128)(2,1)} %bitcast.269), kind=kOutput, calls=%fused_computation.339 | convolution fusion | flops 268435456 | bytes 8781824 | tf_op jit(solution)/shard_map/dot_general | solution.py:92
  296.7 3.5 convolution_convert_fusion.4
  300.2 0.7 copy.142
  301.0 4.4 all-to-all-start.7
  305.9 4.5 all-to-all-done.7
  310.5 4.0 collective-permute-start.2
  314.6 1.2 collective-permute-done.2
  315.8 9.2 %all_to_all.94 = bf16[4,32,1024]{2,1,0:T(8,128)(2,1)S(1)} all-to-all(bf16[4,32,1024]{2,1,0:T(8,128)(2,1)S(1)} %broadcast_in_dim.103), channel_id=1, replica_groups=mesh['seq'=32,'section'=4,'tp'=4] {'tp'}, dimensions={0} | all-to-all | bytes 524288 | tf_op jit(solution)/shard_map/all_to_all | solution.py:24
  325.7 6.0 %fusion.152 = f32[32,8,128]{2,0,1:T(8,128)S(1)} fusion(bf16[32,4096,1]{1,0,2:T(8,128)(2,1)S(1)} %reshape.1100, bf16[8,128,4096]{2,1,0:T(8,128)(2,1)} %bitcast.270), kind=kOutput, calls=%fused_computation.340 | convolution fusion | flops 268435456 | bytes 8781824 | tf_op jit(solution)/shard_map/dot_general | solution.py:92
  332.7 3.5 convolution_convert_fusion.3
  336.2 0.7 copy.141
  337.0 4.4 all-to-all-start.9
  342.0 4.5 all-to-all-done.9
  346.5 4.0 collective-permute-start.3
  350.6 1.2 collective-permute-done.3
  351.9 9.2 %all_to_all.95 = bf16[4,32,1024]{2,1,0:T(8,128)(2,1)S(1)} all-to-all(bf16[4,32,1024]{2,1,0:T(8,128)(2,1)S(1)} %broadcast_in_dim.105), channel_id=1, replica_groups=mesh['seq'=32,'section'=4,'tp'=4] {'tp'}, dimensions={0} | all-to-all | bytes 524288 | tf_op jit(solution)/shard_map/all_to_all | solution.py:24
  361.8 6.0 %fusion.153 = f32[32,8,128]{2,0,1:T(8,128)S(1)} fusion(bf16[32,4096,1]{1,0,2:T(8,128)(2,1)S(1)} %reshape.1103, bf16[8,128,4096]{2,1,0:T(8,128)(2,1)} %bitcast.271), kind=kOutput, calls=%fused_computation.341 | convolution fusion | flops 268435456 | bytes 8781824 | tf_op jit(solution)/shard_map/dot_general | solution.py:92
  368.8 3.5 convolution_convert_fusion.2
  373.0 4.4 all-to-all-start.11
  377.8 4.7 %all-to-all-done.11 = bf16[4,32,1024]{2,1,0:T(8,128)(2,1)S(1)} async-done(((bf16[4,32,1024]{2,1,0:T(8,128)(2,1)}), bf16[4,32,1024]{2,1,0:T(8,128)(2,1)S(1)}, u32[]{:S(2)}, u32[]{:S(2)}) %all-to-all-start.11) | async-done | bytes 262176 | tf_op jit(solution)/shard_map/all_to_all | solution.py:38
  382.5 4.0 collective-permute-start.4
  386.7 1.2 collective-permute-done.4
  387.9 9.2 %all_to_all.96 = bf16[4,32,1024]{2,1,0:T(8,128)(2,1)S(1)} all-to-all(bf16[4,32,1024]{2,1,0:T(8,128)(2,1)S(1)} %broadcast_in_dim.107), channel_id=1, replica_groups=mesh['seq'=32,'section'=4,'tp'=4] {'tp'}, dimensions={0} | all-to-all | bytes 524288 | tf_op jit(solution)/shard_map/all_to_all | solution.py:24
  397.8 6.0 %fusion.154 = f32[32,8,128]{2,0,1:T(8,128)S(1)} fusion(bf16[32,4096,1]{1,0,2:T(8,128)(2,1)S(1)} %reshape.1106, bf16[8,128,4096]{2,1,0:T(8,128)(2,1)} %bitcast.272), kind=kOutput, calls=%fused_computation.342 | convolution fusion | flops 268435456 | bytes 8781824 | tf_op jit(solution)/shard_map/dot_general | solution.py:92
  404.8 3.5 convolution_convert_fusion.1
  409.0 4.4 all-to-all-start.13
  413.8 4.7 %all-to-all-done.13 = bf16[4,32,1024]{2,1,0:T(8,128)(2,1)S(1)} async-done(((bf16[4,32,1024]{2,1,0:T(8,128)(2,1)}), bf16[4,32,1024]{2,1,0:T(8,128)(2,1)S(1)}, u32[]{:S(2)}, u32[]{:S(2)}) %all-to-all-start.13) | async-done | bytes 262176 | tf_op jit(solution)/shard_map/all_to_all | solution.py:38
  418.6 4.0 collective-permute-start.5
  422.7 1.2 collective-permute-done.5
  423.9 9.2 %all_to_all.97 = bf16[4,32,1024]{2,1,0:T(8,128)(2,1)S(1)} all-to-all(bf16[4,32,1024]{2,1,0:T(8,128)(2,1)S(1)} %broadcast_in_dim.110), channel_id=1, replica_groups=mesh['seq'=32,'section'=4,'tp'=4] {'tp'}, dimensions={0} | all-to-all | bytes 524288 | tf_op jit(solution)/shard_map/all_to_all | solution.py:24
  433.8 6.0 %fusion.155 = f32[32,8,128]{2,0,1:T(8,128)S(1)} fusion(bf16[32,4096,1]{1,0,2:T(8,128)(2,1)S(1)} %reshape.1109, bf16[8,128,4096]{2,1,0:T(8,128)(2,1)} %bitcast.273), kind=kOutput, calls=%fused_computation.343 | convolution fusion | flops 268435456 | bytes 8781824 | tf_op jit(solution)/shard_map/dot_general | solution.py:92
  440.8 3.5 convolution_convert_fusion
  445.0 4.4 all-to-all-start.15
  449.8 4.7 %all-to-all-done.15 = bf16[4,32,1024]{2,1,0:T(8,128)(2,1)S(1)} async-done(((bf16[4,32,1024]{2,1,0:T(8,128)(2,1)}), bf16[4,32,1024]{2,1,0:T(8,128)(2,1)S(1)}, u32[]{:S(2)}, u32[]{:S(2)}) %all-to-all-start.15) | async-done | bytes 262176 | tf_op jit(solution)/shard_map/all_to_all | solution.py:38
  454.6 1.5 select_n.303
  (180 shorter events, 22.0 us)
Async XLA Ops:
  6.5 192.6 %all-gather.2.cloned.1.call-start = ((), (), s32[]{:S(2)}) async-start(), calls=%async_computation.16 | async-start | bytes 12976128 | tf_op jit(solution)/shard_map/all_gather | solution.py:54
  9.7 30.3 %all-to-all-start = ((s32[32,1,64]{2,1,0:T(1,128)}), s32[32,1,64]{2,1,0:T(1,128)S(1)}, u32[]{:S(2)}, u32[]{:S(2)}) async-start(s32[32,1,64]{2,1,0:T(1,128)} %broadcast_in_dim.89), calls=%async_computation | async-start | bytes 32768 | tf_op jit(solution)/shard_map/all_to_all | solution.py:24
  40.0 47.6 %copy-start.1 = (bf16[1,4096]{1,0:T(2,128)(2,1)S(1)}, bf16[1,4096]{1,0:T(2,128)(2,1)}, u32[]{:S(2)}) copy-start(bf16[1,4096]{1,0:T(2,128)(2,1)} %param.7) | copy-start | bytes 24580
  56.1 23.4 %all-to-all-start.1 = ((bf16[32,32,128]{2,0,1:T(8,128)(2,1)}), bf16[32,32,128]{2,0,1:T(8,128)(2,1)S(1)}, u32[]{:S(2)}, u32[]{:S(2)}) async-start(bf16[32,32,128]{2,0,1:T(8,128)(2,1)} %pad_maximum_fusion.1), calls=%async_computation.1 | async-start | bytes 524288 | tf_op jit(solution)/shard_map/all_to_all | solution.py:154
  80.9 40.6 %all-to-all-start.2 = ((bf16[4,32,1024]{2,1,0:T(8,128)(2,1)}), bf16[4,32,1024]{2,1,0:T(8,128)(2,1)S(1)}, u32[]{:S(2)}, u32[]{:S(2)}) async-start(bf16[4,32,1024]{2,1,0:T(8,128)(2,1)} %broadcast_in_dim.95), calls=%async_computation.2 | async-start | bytes 524288 | tf_op jit(solution)/shard_map/all_to_all | solution.py:24
  229.2 10.0 %all-to-all-start.3 = ((bf16[4,32,1024]{2,1,0:T(8,128)(2,1)}), bf16[4,32,1024]{2,1,0:T(8,128)(2,1)S(1)}, u32[]{:S(2)}, u32[]{:S(2)}) async-start(bf16[4,32,1024]{2,1,0:T(8,128)(2,1)} %bitcast.266), calls=%async_computation.3 | async-start | bytes 524288 | tf_op jit(solution)/shard_map/all_to_all | solution.py:38
  239.3 4.4 collective-permute-start
  264.9 9.5 %all-to-all-start.5 = ((bf16[4,32,1024]{2,1,0:T(8,128)(2,1)}), bf16[4,32,1024]{2,1,0:T(8,128)(2,1)S(1)}, u32[]{:S(2)}, u32[]{:S(2)}) async-start(bf16[4,32,1024]{2,1,0:T(8,128)(2,1)} %bitcast.264), calls=%async_computation.5 | async-start | bytes 524288 | tf_op jit(solution)/shard_map/all_to_all | solution.py:38
  274.5 5.3 %collective-permute-start.1 = (bf16[32,1024]{1,0:T(8,128)(2,1)S(1)}, bf16[32,1024]{1,0:T(8,128)(2,1)S(1)}, u32[]{:S(2)}, u32[]{:S(2)}) collective-permute-start(bf16[32,1024]{1,0:T(8,128)(2,1)S(1)} %get-tuple-element.14), channel_id=1, source_target_pairs={{0,4},{4,8},{8,12},{1,5},{5,9},{9,13},{2,6},{6,10},{10,14},{3,7},{... | collective-permute-start | bytes 196616 | tf_op jit(solution)/shard_map/ppermute | solution.py:45
  301.0 9.4 %all-to-all-start.7 = ((bf16[4,32,1024]{2,1,0:T(8,128)(2,1)}), bf16[4,32,1024]{2,1,0:T(8,128)(2,1)S(1)}, u32[]{:S(2)}, u32[]{:S(2)}) async-start(bf16[4,32,1024]{2,1,0:T(8,128)(2,1)} %bitcast.262), calls=%async_computation.7 | async-start | bytes 524288 | tf_op jit(solution)/shard_map/all_to_all | solution.py:38
  310.5 5.3 %collective-permute-start.2 = (bf16[32,1024]{1,0:T(8,128)(2,1)S(1)}, bf16[32,1024]{1,0:T(8,128)(2,1)S(1)}, u32[]{:S(2)}, u32[]{:S(2)}) collective-permute-start(bf16[32,1024]{1,0:T(8,128)(2,1)S(1)} %get-tuple-element.12), channel_id=1, source_target_pairs={{0,4},{4,8},{8,12},{1,5},{5,9},{9,13},{2,6},{6,10},{10,14},{3,7},{... | collective-permute-start | bytes 196616 | tf_op jit(solution)/shard_map/ppermute | solution.py:45
  337.0 9.4 %all-to-all-start.9 = ((bf16[4,32,1024]{2,1,0:T(8,128)(2,1)}), bf16[4,32,1024]{2,1,0:T(8,128)(2,1)S(1)}, u32[]{:S(2)}, u32[]{:S(2)}) async-start(bf16[4,32,1024]{2,1,0:T(8,128)(2,1)} %bitcast.260), calls=%async_computation.9 | async-start | bytes 524288 | tf_op jit(solution)/shard_map/all_to_all | solution.py:38
  346.5 5.3 %collective-permute-start.3 = (bf16[32,1024]{1,0:T(8,128)(2,1)S(1)}, bf16[32,1024]{1,0:T(8,128)(2,1)S(1)}, u32[]{:S(2)}, u32[]{:S(2)}) collective-permute-start(bf16[32,1024]{1,0:T(8,128)(2,1)S(1)} %get-tuple-element.10), channel_id=1, source_target_pairs={{0,4},{4,8},{8,12},{1,5},{5,9},{9,13},{2,6},{6,10},{10,14},{3,7},{... | collective-permute-start | bytes 196616 | tf_op jit(solution)/shard_map/ppermute | solution.py:45
  373.0 9.4 %all-to-all-start.11 = ((bf16[4,32,1024]{2,1,0:T(8,128)(2,1)}), bf16[4,32,1024]{2,1,0:T(8,128)(2,1)S(1)}, u32[]{:S(2)}, u32[]{:S(2)}) async-start(bf16[4,32,1024]{2,1,0:T(8,128)(2,1)} %bitcast.258), calls=%async_computation.11 | async-start | bytes 524288 | tf_op jit(solution)/shard_map/all_to_all | solution.py:38
  382.5 5.3 %collective-permute-start.4 = (bf16[32,1024]{1,0:T(8,128)(2,1)S(1)}, bf16[32,1024]{1,0:T(8,128)(2,1)S(1)}, u32[]{:S(2)}, u32[]{:S(2)}) collective-permute-start(bf16[32,1024]{1,0:T(8,128)(2,1)S(1)} %get-tuple-element.8), channel_id=1, source_target_pairs={{0,4},{4,8},{8,12},{1,5},{5,9},{9,13},{2,6},{6,10},{10,14},{3,7},{... | collective-permute-start | bytes 196616 | tf_op jit(solution)/shard_map/ppermute | solution.py:45
  409.0 9.4 %all-to-all-start.13 = ((bf16[4,32,1024]{2,1,0:T(8,128)(2,1)}), bf16[4,32,1024]{2,1,0:T(8,128)(2,1)S(1)}, u32[]{:S(2)}, u32[]{:S(2)}) async-start(bf16[4,32,1024]{2,1,0:T(8,128)(2,1)} %bitcast.256), calls=%async_computation.13 | async-start | bytes 524288 | tf_op jit(solution)/shard_map/all_to_all | solution.py:38
  418.6 5.3 %collective-permute-start.5 = (bf16[32,1024]{1,0:T(8,128)(2,1)S(1)}, bf16[32,1024]{1,0:T(8,128)(2,1)S(1)}, u32[]{:S(2)}, u32[]{:S(2)}) collective-permute-start(bf16[32,1024]{1,0:T(8,128)(2,1)S(1)} %get-tuple-element.6), channel_id=1, source_target_pairs={{0,4},{4,8},{8,12},{1,5},{5,9},{9,13},{2,6},{6,10},{10,14},{3,7},{... | collective-permute-start | bytes 196616 | tf_op jit(solution)/shard_map/ppermute | solution.py:45
  445.0 9.4 %all-to-all-start.15 = ((bf16[4,32,1024]{2,1,0:T(8,128)(2,1)}), bf16[4,32,1024]{2,1,0:T(8,128)(2,1)S(1)}, u32[]{:S(2)}, u32[]{:S(2)}) async-start(bf16[4,32,1024]{2,1,0:T(8,128)(2,1)} %bitcast.254), calls=%async_computation.15 | async-start | bytes 524288 | tf_op jit(solution)/shard_map/all_to_all | solution.py:38
  449.8 4.8 %copy-start = (bf16[64,1024]{1,0:T(8,128)(2,1)}, bf16[64,1024]{1,0:T(8,128)(2,1)S(1)}, u32[]{:S(2)}) copy-start(bf16[64,1024]{1,0:T(8,128)(2,1)S(1)} %select_n.295) | copy-start | bytes 393220
Sparse Core Ops, SparseCore 0:
  10.5 188.5 all-gather.1
where the time goes:
time: 466 us; the launch traced here: 463 us
  waiting for transfers between devices  161 us (35%)
  starting transfers between devices  89.4 us (19%)
  matrix products  69.5 us (15%)
  local copies, waits for them, and re-layouts  63.2 us (14%)
  blocking collectives  55.2 us (12%)
  between operations  14.4 us (3%)
  other arithmetic  10.1 us (2%)
    all_gather x1, waiting for transfers between devices, sent_together(): lax.all_gather(both, axis, axis=dim, tiled=True)  76.9 us
    all_to_all x6, blocking collectives, sent_to_all(): return lax.all_to_all(copies, axis, split_axis=0, concat_axis=0, tiled=True)  55.2 us
    dot_general x7, matrix products, project(): jnp.dot(normed, qkv_full, preferred_element_type=jnp.float32)  41.7 us
    all_to_all x2, waiting for transfers between devices, sent_to_all(): return lax.all_to_all(copies, axis, split_axis=0, concat_axis=0, tiled=True)  33.4 us
    all_to_all x7, waiting for transfers between devices, sum_at_owner(): lax.all_to_all(in_blocks(value, dim, length), axis, 0, 0, tiled=True)  32.4 us
    all_to_all x7, starting transfers between devices, sum_at_owner(): lax.all_to_all(in_blocks(value, dim, length), axis, 0, 0, tiled=True)  31.5 us
    dot_general x7, matrix products, combine(): lax.dot_general(attended, out_full, (((1,), (1,)), ((), ())), preferred_e...  24.5 us
    all_to_all x2, starting transfers between devices, sent_to_all(): return lax.all_to_all(copies, axis, split_axis=0, concat_axis=0, tiled=True)  23.2 us
  transfers between devices with their start and end apart: 17, of which 16 were waited for; matrix products, arithmetic and copies ran while one was open for 8% of the time, Pallas kernels for 0%

commit v1 on v0

v1 whole, which is shorter than its diff:
```python
import functools

import jax
import jax.numpy as jnp
import numpy as np
from jax import lax
from jax.experimental import pallas as pl
from jax.experimental.pallas import tpu as pltpu
from jax.sharding import PartitionSpec as P

MESH = pl.DeviceIdType.MESH
LAYERS = 4
NY = 8
NZ = 4
SEQ = NY * NZ
GROUP = 8
ROWS = 128
BLOCK = 64
HEAD = 128
WIDE = 768
SLICE = 512
EPS = 1e-05
ROPE_BASE = 500000.0
MASKED = -1e30
Z_STEPS = (0, 1, 3, 2)


def remote(src, dst, send, recv, seq, section, tp):
    return pltpu.make_async_remote_copy(
        src_ref=src,
        dst_ref=dst,
        send_sem=send,
        recv_sem=recv,
        device_id=(seq, section, tp),
        device_id_type=MESH,
    )


def kernel(
    ids_ref, table_ref, wsrc_ref, rope_a_ref, rope_b_ref, out_ref,
    w, tab, ids_v, ids_s, emb_out, emb_in, hid, part_out, part_in, kv, akv, acc, res,
    x_send, x_recv, z_send, z_recv, y_send, y_recv, push_send, push_recv,
    ids_send, ids_recv, ids_local, tab_sem, emb_send, emb_recv,
    ag_send, ag_recv, rs_send, rs_recv, kv_send, kv_recv, out_send, out_recv,
):
    seq = lax.axis_index("seq")
    x = lax.axis_index("section")
    tp = lax.axis_index("tp")
    y = seq // NZ
    zh = seq % NZ
    zl = tp // 2
    c = tp % 2
    m = 4 * zl + x
    comm = 2 * zl
    chain = 2 * zl + 1
    is_comm = c == 0
    is_chain = c == 1

    def x_copy(j):
        return remote(
            wsrc_ref.at[j], w.at[x, seq], x_send.at[j], x_recv.at[x], seq, 2 * c + j, comm
        )

    for j in range(2):
        stays = is_comm & (x == j)

        @pl.when(jnp.logical_not(stays))
        def _():
            x_copy(j).start()

        @pl.when(stays)
        def _():
            w[x, seq] = wsrc_ref[j]

    @pl.loop(0, tab.shape[0])
    def _(k):
        columns = pl.ds(pl.multiple_of(k * HEAD, HEAD), HEAD)
        pltpu.make_async_copy(table_ref.at[:, columns], tab.at[k], tab_sem).start()

    def ids_copy(d):
        return remote(
            ids_ref, ids_v.at[y], ids_send.at[d], ids_recv.at[y], (seq + d) % SEQ, x, tp
        )

    @pl.when(zh == x)
    def _():
        @pl.loop(1, SEQ)
        def _(d):
            ids_copy(d).start()

        ids_v[y] = ids_ref[...]

    def z_copy(layer, dz):
        return remote(
            w.at[layer, seq], w.at[layer, seq], z_send.at[layer], z_recv.at[layer, dz],
            NZ * y + (zh + dz) % NZ, x, comm,
        )

    def push(layer, s):
        remote(
            w.at[layer, s], w.at[layer, s], push_send.at[layer], push_recv.at[layer], seq, x, chain
        ).start()

    def y_copy(layer, way, step, zi, s):
        to = (seq + (NZ if way == 0 else SEQ - NZ)) % SEQ
        return remote(
            w.at[layer, s], w.at[layer, s], y_send.at[layer, way], y_recv.at[layer, way, step, zi],
            to, x, comm,
        )

    @pl.when(is_comm)
    def _():
        for layer in range(LAYERS):
            local = (x == layer) & (x < 2)

            @pl.when(jnp.logical_not(local))
            def _():
                remote(
                    w.at[layer, seq], w.at[layer, seq], x_send.at[0], x_recv.at[layer], seq, x, comm
                ).wait_recv()

            for dz in (1, 3, 2):
                z_copy(layer, dz).start()
            if layer == 0:
                for way in range(2):
                    y_copy(0, way, 0, 0, seq).start()
            push(layer, seq)

    @pl.loop(0, NY)
    def _(b):
        @pl.when(jnp.logical_not((zh == x) & (b == y)))
        def _():
            remote(
                ids_ref, ids_v.at[b], ids_send.at[0], ids_recv.at[b], seq, x, tp
            ).wait_recv()

    to_scalar = pltpu.make_async_copy(ids_v, ids_s, ids_local)
    to_scalar.start()
    to_scalar.wait()
    pltpu.make_async_copy(tab, tab, tab_sem).wait()
    emb_section = 2 * c + seq // 16
    lane = lax.broadcasted_iota(jnp.int32, (32, HEAD), 1)

    def emb_copy(b):
        return remote(
            emb_out.at[b], emb_in.at[seq % 16], emb_send.at[b], emb_recv.at[seq % 16],
            NZ * b + x, emb_section, chain,
        )

    def emb_self(b):
        return is_chain & (emb_section == x) & (NZ * b + x == seq)

    @pl.loop(0, NY)
    def _(b):
        def token(i, got):
            v = ids_s[b, 0, i]
            tile = tab[v >> 7].astype(jnp.float32)
            column = jnp.sum(jnp.where(lane == (v & 127), tile, 0.0), axis=1, keepdims=True)
            return jnp.where(lane == i, column, got)

        got = lax.fori_loop(0, BLOCK, token, jnp.zeros((32, HEAD), jnp.float32), unroll=8)
        emb_out[b] = got.astype(jnp.bfloat16)

        @pl.when(jnp.logical_not(emb_self(b)))
        def _():
            emb_copy(b).start()

        @pl.when(emb_self(b))
        def _():
            emb_in[seq % 16] = got.astype(jnp.bfloat16)

    def own_sends(layer, first):
        for zi in range(first, NZ):
            dz = Z_STEPS[zi]
            s = NZ * y + (zh + NZ - dz) % NZ
            if zi > 0:
                remote(
                    w.at[layer, s], w.at[layer, s], z_send.at[layer], z_recv.at[layer, dz],
                    seq, x, comm,
                ).wait_recv()
            for way in range(2):
                y_copy(layer, way, 0, zi, s).start()
            if zi > 0:
                push(layer, s)

    def received(way, step, zi):
        row = (y + (NY - step if way == 0 else step)) % NY
        return NZ * row + (zh + NZ - Z_STEPS[zi]) % NZ

    def arrived(layer, way, step, zi):
        s = received(way, step, zi)
        y_copy(layer, way, step - 1, zi, s).wait_recv()
        return s

    @pl.when(is_comm)
    def _():
        own_sends(0, 1)

        @pl.loop(0, LAYERS)
        def _(layer):
            for step in range(1, 4):
                for zi in range(NZ):
                    for way in range(2):
                        s = arrived(layer, way, step, zi)
                        if step < 3 or (zi < 2) == (way == 0):
                            y_copy(layer, way, step, zi, s).start()
                        push(layer, s)

            @pl.when(layer < LAYERS - 1)
            def _():
                own_sends(layer + 1, 0)

            for zi in range(NZ):
                push(layer, arrived(layer, 0 if zi < 2 else 1, 4, zi))

        @pl.loop(0, LAYERS)
        def _(layer):
            for way in range(2):
                remote(
                    w.at[layer, pl.ds(0, 14)], w.at[layer, pl.ds(0, 14)], y_send.at[layer, way],
                    y_recv.at[layer, way, 0, 0], seq, x, comm,
                ).wait_send()
            remote(
                w.at[layer, pl.ds(0, 3)], w.at[layer, pl.ds(0, 3)], z_send.at[layer],
                z_recv.at[layer, 1], seq, x, comm,
            ).wait_send()
            remote(
                w.at[layer], w.at[layer], push_send.at[layer], push_recv.at[layer], seq, x, chain
            ).wait_send()

    def member(d):
        other = m ^ d
        return other, other % 4, 2 * (other // 4) + 1

    def ag_copy(layer, d):
        _, section, to = member(d)
        return remote(
            hid.at[layer, m], hid.at[layer, m], ag_send.at[layer], ag_recv.at[layer, m],
            seq, section, to,
        )

    def rs_copy(layer, d):
        other, section, to = member(d)
        return remote(
            part_out.at[layer, other], part_in.at[layer, m], rs_send.at[layer],
            rs_recv.at[layer, m], seq, section, to,
        )

    def kv_copy(layer, src, i, to):
        return remote(src, akv.at[layer], kv_send.at[layer, i], kv_recv.at[layer], to, x, tp)

    def out_copy(layer):
        return remote(
            hid.at[layer + 1, m], out_ref.at[:, pl.ds(pl.multiple_of((x % 2) * SLICE, SLICE), SLICE)],
            out_send.at[layer], out_recv.at[x % 2], seq, layer, 2 * zl + x // 2,
        )

    def out_self(layer):
        return (layer == x) & (x >= 2)

    @pl.when(is_chain)
    def _():
        self_emb = (zh == x) & (x >= 2) & (seq // 16 == x % 2)

        @pl.loop(0, 16)
        def _(k):
            @pl.when(jnp.logical_not(self_emb & (k == seq % 16)))
            def _():
                remote(
                    emb_out.at[0], emb_in.at[k], emb_send.at[0], emb_recv.at[k], seq, x, tp
                ).wait_recv()

        start = emb_in[...].reshape(SLICE, HEAD).astype(jnp.float32).T[:BLOCK]
        res[...] = start
        hid[0, m] = start.astype(jnp.bfloat16)
        for d in range(1, GROUP):
            ag_copy(0, d).start()

        a = rope_a_ref[pl.ds(seq, 1), :]
        cos_a, sin_a = a[:, :HEAD], a[:, HEAD:]
        cos_b, sin_b = rope_b_ref[:, :HEAD], rope_b_ref[:, HEAD:]
        cosine = cos_a * cos_b - sin_a * sin_b
        sine = sin_a * cos_b + cos_a * sin_b
        side = lax.broadcasted_iota(jnp.int32, (BLOCK, HEAD), 1)
        sine = jnp.where(side < HEAD // 2, -sine, sine)

        def rotated(v):
            return (v * cosine + pltpu.roll(v, HEAD // 2, 1) * sine).astype(jnp.bfloat16)

        row = lax.broadcasted_iota(jnp.int32, (2 * BLOCK, 2 * BLOCK), 0) % BLOCK
        col = lax.broadcasted_iota(jnp.int32, (2 * BLOCK, 2 * BLOCK), 1)
        allowed = ((col < BLOCK) & (seq > 0)) | ((col >= BLOCK) & (col - BLOCK <= row))

        @pl.loop(0, LAYERS)
        def _(layer):
            remote(
                w.at[layer], w.at[layer], push_send.at[layer], push_recv.at[layer], seq, x, chain
            ).wait_recv()

            def add(d, square):
                other = m ^ d

                @pl.when(d > 0)
                def _():
                    remote(
                        hid.at[layer, other], hid.at[layer, other], ag_send.at[layer],
                        ag_recv.at[layer, other], seq, x, chain,
                    ).wait_recv()

                h = hid[layer, other]
                weights = w[layer, pl.ds(4 * other, 4), :, :SLICE].reshape(SLICE, SLICE)
                product = jnp.dot(h, weights, preferred_element_type=jnp.float32)

                @pl.when(d == 0)
                def _():
                    acc[...] = product

                @pl.when(d > 0)
                def _():
                    acc[...] += product

                hf = h.astype(jnp.float32)
                return square + jnp.sum(hf * hf, axis=1, keepdims=True)

            square = lax.fori_loop(0, GROUP, add, jnp.zeros((BLOCK, 1), jnp.float32))
            projected = acc[...] * lax.rsqrt(square * (1.0 / (GROUP * SLICE)) + EPS)
            q0 = rotated(projected[:, :HEAD])
            q1 = rotated(projected[:, HEAD : 2 * HEAD])
            key = rotated(projected[:, 2 * HEAD : 3 * HEAD])
            value = projected[:, 3 * HEAD :].astype(jnp.bfloat16)
            kv[layer, :, :HEAD] = key
            kv[layer, :, HEAD:] = value

            @pl.when(seq == 0)
            def _():
                for i in range(1, NY):
                    kv_copy(layer, kv.at[layer], i, NZ * i).start()
                for i in range(1, NZ):
                    kv_copy(layer, kv.at[layer], NY + i, i).start()
                akv[layer, :, :HEAD] = key
                akv[layer, :, HEAD:] = value

            @pl.when(seq > 0)
            def _():
                kv_copy(layer, kv.at[layer], 0, seq).wait_recv()

                @pl.when(zh == 0)
                def _():
                    for i in range(1, NZ):
                        kv_copy(layer, akv.at[layer], NY + i, seq + i).start()

            queries = jnp.concatenate([q0, q1], axis=0)
            keys = jnp.concatenate([akv[layer, :, :HEAD], key], axis=0)
            values = jnp.concatenate([akv[layer, :, HEAD:], value], axis=0)
            scores = lax.dot_general(
                queries, keys, (((1,), (1,)), ((), ())), preferred_element_type=jnp.float32
            ) * (HEAD ** -0.5)
            scores = jnp.where(allowed, scores, MASKED)
            e = jnp.exp(scores - jnp.max(scores, axis=1, keepdims=True))
            probs = (e / jnp.sum(e, axis=1, keepdims=True)).astype(jnp.bfloat16)
            both = jnp.dot(probs, values, preferred_element_type=jnp.float32).astype(jnp.bfloat16)
            attended = jnp.concatenate([both[:BLOCK], both[BLOCK:]], axis=1)

            def partial(other):
                weights = w[layer, pl.ds(4 * other, 4), :, SLICE:].reshape(SLICE, 2 * HEAD)
                return lax.dot_general(
                    attended, weights, (((1,), (1,)), ((), ())), preferred_element_type=jnp.float32
                )

            @pl.loop(1, GROUP)
            def _(d):
                other = m ^ d
                part_out[layer, other] = partial(other).astype(jnp.bfloat16)
                rs_copy(layer, d).start()

            acc[...] = partial(m)

            @pl.loop(1, GROUP)
            def _(d):
                other = m ^ d
                remote(
                    part_out.at[layer, other], part_in.at[layer, other], rs_send.at[layer],
                    rs_recv.at[layer, other], seq, x, chain,
                ).wait_recv()
                acc[...] += part_in[layer, other].astype(jnp.float32)

            new = (res[...] + acc[...]).astype(jnp.bfloat16)
            res[...] = new.astype(jnp.float32)
            hid[layer + 1, m] = new

            @pl.when(layer < LAYERS - 1)
            def _():
                for d in range(1, GROUP):
                    ag_copy(layer + 1, d).start()

            @pl.when(jnp.logical_not(out_self(layer)))
            def _():
                out_copy(layer).start()

            @pl.when(out_self(layer))
            def _():
                out_ref[:, pl.ds(pl.multiple_of((x % 2) * SLICE, SLICE), SLICE)] = new

        @pl.loop(0, LAYERS)
        def _(layer):
            remote(
                hid.at[layer, pl.ds(0, 7)], hid.at[layer, pl.ds(0, 7)], ag_send.at[layer],
                ag_recv.at[layer, 0], seq, x, chain,
            ).wait_send()
            remote(
                part_out.at[layer, pl.ds(0, 7)], part_in.at[layer, pl.ds(0, 7)], rs_send.at[layer],
                rs_recv.at[layer, 0], seq, x, chain,
            ).wait_send()

            @pl.when(seq == 0)
            def _():
                for i in range(1, NY):
                    kv_copy(layer, kv.at[layer], i, seq).wait_send()

            @pl.when(zh == 0)
            def _():
                for i in range(1, NZ):
                    kv_copy(layer, kv.at[layer], NY + i, seq).wait_send()

            @pl.when(jnp.logical_not(out_self(layer)))
            def _():
                out_copy(layer).wait_send()

    for j in range(2):
        @pl.when(jnp.logical_not(is_comm & (x == j)))
        def _():
            x_copy(j).wait_send()

    @pl.when(zh == x)
    def _():
        @pl.loop(1, SEQ)
        def _(d):
            ids_copy(d).wait_send()

    @pl.loop(0, NY)
    def _(b):
        @pl.when(jnp.logical_not(emb_self(b)))
        def _():
            emb_copy(b).wait_send()

    for half in range(2):
        @pl.when(jnp.logical_not(is_chain & (x == 2 + half)))
        def _():
            remote(
                hid.at[0, 0], out_ref.at[:, pl.ds(half * SLICE, SLICE)], out_send.at[0],
                out_recv.at[half], seq, x, tp,
            ).wait_recv()


def rope_constants():
    half = np.arange(HEAD // 2, dtype=np.float64)
    freq = np.float64(ROPE_BASE) ** (-2.0 * half / HEAD)
    freq = np.concatenate([freq, freq])
    coarse = np.arange(SEQ, dtype=np.float64)[:, None] * BLOCK * freq[None]
    fine = np.arange(BLOCK, dtype=np.float64)[:, None] * freq[None]
    pair = lambda angle: np.concatenate([np.cos(angle), np.sin(angle)], axis=1).astype(np.float32)
    return pair(coarse), pair(fine)


def body(token_ids, embed_columns, norm_gain, qkv_weight, out_weight):
    seq = lax.axis_index("seq")
    ids = jnp.broadcast_to(jnp.pad(token_ids, (0, HEAD - BLOCK))[None], (8, HEAD))
    gain = lax.dynamic_slice_in_dim(norm_gain[0], seq * ROWS, ROWS, 0).astype(jnp.float32)
    qkv = (qkv_weight[0].astype(jnp.float32) * gain[:, None]).astype(jnp.bfloat16)
    out = out_weight[0]
    pieces = [
        jnp.concatenate(
            [
                qkv[:, 2 * HEAD * j : 2 * HEAD * (j + 1)],
                qkv[:, HEAD * (4 + j) : HEAD * (5 + j)],
                qkv[:, HEAD * (6 + j) : HEAD * (7 + j)],
                out[:, 2 * HEAD * j : 2 * HEAD * (j + 1)],
            ],
            axis=1,
        )
        for j in range(2)
    ]
    sources = jnp.stack(pieces)
    rope_a, rope_b = rope_constants()
    bf16, f32 = jnp.bfloat16, jnp.float32
    vmem = pl.BlockSpec(memory_space=pltpu.VMEM)
    dma = pltpu.SemaphoreType.DMA
    states = pl.pallas_call(
        kernel,
        out_shape=jax.ShapeDtypeStruct((BLOCK, 2 * SLICE), bf16),
        in_specs=[vmem, pl.BlockSpec(memory_space=pl.ANY), vmem, vmem, vmem],
        out_specs=vmem,
        scratch_shapes=[
            pltpu.VMEM((LAYERS, SEQ, ROWS, WIDE), bf16),
            pltpu.VMEM((embed_columns.shape[1] // HEAD, 32, HEAD), bf16),
            pltpu.VMEM((NY, 8, HEAD), jnp.int32),
            pltpu.SMEM((NY, 8, HEAD), jnp.int32),
            pltpu.VMEM((NY, 32, HEAD), bf16),
            pltpu.VMEM((16, 32, HEAD), bf16),
            pltpu.VMEM((LAYERS + 1, GROUP, BLOCK, SLICE), bf16),
            pltpu.VMEM((LAYERS, GROUP, BLOCK, SLICE), bf16),
            pltpu.VMEM((LAYERS, GROUP, BLOCK, SLICE), bf16),
            pltpu.VMEM((LAYERS, BLOCK, 2 * HEAD), bf16),
            pltpu.VMEM((LAYERS, BLOCK, 2 * HEAD), bf16),
            pltpu.VMEM((BLOCK, SLICE), f32),
            pltpu.VMEM((BLOCK, SLICE), f32),
            dma((2,)),
            dma((LAYERS,)),
            dma((LAYERS,)),
            dma((LAYERS, NZ)),
            dma((LAYERS, 2)),
            dma((LAYERS, 2, 4, NZ)),
            dma((LAYERS,)),
            dma((LAYERS,)),
            dma((SEQ,)),
            dma((NY,)),
            dma,
            dma,
            dma((NY,)),
            dma((16,)),
            dma((LAYERS,)),
            dma((LAYERS, GROUP)),
            dma((LAYERS,)),
            dma((LAYERS, GROUP)),
            dma((LAYERS, NY + NZ)),
            dma((LAYERS,)),
            dma((LAYERS,)),
            dma((2,)),
        ],
        compiler_params=pltpu.CompilerParams(
            has_side_effects=True, vmem_limit_bytes=62 * 1024 * 1024
        ),
    )(ids, embed_columns, sources, jnp.asarray(rope_a), jnp.asarray(rope_b))
    return states[None]


def solution(mesh):
    placed = (
        P("seq"),
        P(("tp", "seq"), None),
        P("section", None),
        P("section", "seq", "tp"),
        P("section", "seq", "tp"),
    )
    return jax.shard_map(
        body, mesh=mesh, in_specs=placed, out_specs=P("section", "seq", "tp"), check_vma=False
    )
```

time: 466 us -> 199 us (0.43)
  Pallas kernels: 0 us -> 190 us
  waiting for transfers between devices: 161 us -> 0 us
  starting transfers between devices: 89.4 us -> 0 us
  matrix products: 69.5 us -> 0 us
  local copies, waits for them, and re-layouts: 63.2 us -> 3.74 us
  blocking collectives: 55.2 us -> 0 us
  between operations: 14.4 us -> 0.04 us
  other arithmetic: 10.1 us -> 2.54 us
    pallas_call x0 -> x1, Pallas kernels: none -> 190 us  [body(): pl.pallas_call(kernel, out_shape=jax.ShapeDtypeStruct((BLOCK, 2 * SLICE),...]
    all_to_all x10 -> x0, waiting for transfers between devices: 77.2 us -> none  [the longest x2 33.4 us: sent_to_all(): return lax.all_to_all(copies, axis, split_axis=0, concat_axis=0, tiled=True)]
    all_gather x1 -> x0, waiting for transfers between devices: 76.9 us -> none  [sent_together(): lax.all_gather(both, axis, axis=dim, tiled=True)]
    dot_general x28 -> x0, matrix products: 69.5 us -> none  [the longest x7 41.7 us: project(): jnp.dot(normed, qkv_full, preferred_element_type=jnp.float32)]
    all_to_all x10 -> x0, starting transfers between devices: 66.4 us -> none  [the longest x7 31.5 us: sum_at_owner(): lax.all_to_all(in_blocks(value, dim, length), axis, 0, 0, tiled=True)]
    all_to_all x6 -> x0, blocking collectives: 55.2 us -> none  [sent_to_all(): return lax.all_to_all(copies, axis, split_axis=0, concat_axis=0, tiled=True)]
    ppermute x6 -> x0, starting transfers between devices: 23 us -> none  [passed_along(): lax.ppermute(value, axis, [(source, source + steps) for source in range(l...]
    dot_general x2 -> x0, local copies, waits for them, and re-layouts: 18.8 us -> none  [project(): jnp.dot(normed, qkv_full, preferred_element_type=jnp.float32)]
  transfers between devices with their start and end apart: 17 -> 0, of which waited for: 16 -> 0; matrix products, arithmetic and copies ran while one was open for 8% -> 0% of each run, Pallas kernels for 0% -> 0%
where the time goes in v1:
time: 199 us; the launch traced here: 197 us
  Pallas kernels  190 us (95%)
  local copies, waits for them, and re-layouts  3.74 us (2%)
  other arithmetic  2.54 us (1%)
    pallas_call x1, Pallas kernels, body(): pl.pallas_call(kernel, out_shape=jax.ShapeDtypeStruct((BLOCK, 2 * SLICE),...  190 us

profile of v1, /device:TPU:1, one launch (start us, length us, event | category | flops | bytes accessed | tf_op | source)
XLA Modules:
  0.0 196.6 jit_solution(14676183322418775438)
XLA Ops:
  0.0 0.7 bitcast_convert_fusion
  0.7 1.1 fusion
  1.8 0.9 fusion.3
  2.7 0.8 pad_maximum_fusion.wsrc_ref
  3.5 0.7 pad.4
  4.2 0.6 broadcast_in_dim.4.ids_ref
  4.7 190.3 %shard_map.73 = bf16[64,1024]{1,0:T(8,128)(2,1)} custom-call(s32[8,128]{1,0:T(8,128)} %broadcast_in_dim.4.ids_ref, bf16[32,65536]{1,0:T(8,128)(2,1)} %table_ref.1, bf16[2,128,768]{2,1,0:T(8,128)(2,1)} %pad_maximum_fusion.wsrc_ref, f32[32,256]{1,0:T(8,128)} %constant.17.clone.rope_a_ref, f32[64,256]{1,0:T(8,128)} %constant.18.clone.rope_b_ref), custom_call_target="tpu_custom_call" | custom-call | tf_op jit(solution)/shard_map/pallas_call | solution.py:488
  195.1 1.6 copy.9
  (3 shorter events, 0.1 us)

commit v2 on v1

--- a/solution.py
+++ b/solution.py
@@ -37,8 +37,8 @@
 
 
 def kernel(
-    ids_ref, table_ref, wsrc_ref, rope_a_ref, rope_b_ref, out_ref,
-    w, tab, ids_v, ids_s, emb_out, emb_in, hid, part_out, part_in, kv, akv, acc, res,
+    token_ref, table_ref, gain_ref, qkv_ref, proj_ref, rope_a_ref, rope_b_ref, out_ref,
+    ids_ref, wsrc_ref, w, tab, ids_v, ids_s, emb_out, emb_in, hid, part_out, part_in, kv, akv, acc, res,
     x_send, x_recv, z_send, z_recv, y_send, y_recv, push_send, push_recv,
     ids_send, ids_recv, ids_local, tab_sem, emb_send, emb_recv,
     ag_send, ag_recv, rs_send, rs_recv, kv_send, kv_recv, out_send, out_recv,
@@ -56,10 +56,73 @@
     is_comm = c == 0
     is_chain = c == 1
 
+    table_copy = pltpu.make_async_copy(table_ref, tab, tab_sem)
+    table_copy.start()
+
+    barrier = pltpu.get_barrier_semaphore()
+    emb_section = 2 * c + seq // 16
+    self_emb = is_chain & (zh == x) & (emb_section == x)
+
+    def greet(to_seq, section, to):
+        pl.semaphore_signal(
+            barrier, inc=1, device_id=(to_seq, section, to), device_id_type=MESH
+        )
+
+    with jax.named_scope("greet"):
+        @pl.loop(1, SEQ)
+        def _(d):
+            greet((seq + d) % SEQ, x, tp)
+
+        @pl.loop(1, 16)
+        def _(d):
+            other = (4 * x + tp + d) % 16
+            greet(seq, other // 4, other % 4)
+
+        @pl.loop(0, NY)
+        def _(b):
+            @pl.when(jnp.logical_not(self_emb & (b == y)))
+            def _():
+                greet(NZ * b + x, emb_section, chain)
+
+        @pl.when(is_chain)
+        def _():
+            @pl.loop(0, 16)
+            def _(k):
+                @pl.when(jnp.logical_not(self_emb & (k == seq % 16)))
+                def _():
+                    greet(16 * (x % 2) + k, zh, 2 * zl + x // 2)
+
+    gain = gain_ref[:, pl.ds(pl.multiple_of(seq * ROWS, ROWS), ROWS)].astype(jnp.float32)
+    gain = jnp.broadcast_to(gain, (ROWS, ROWS)).T
+
+    def scaled(start):
+        heads = qkv_ref[:, start : start + HEAD].astype(jnp.float32)
+        return (heads * gain).astype(jnp.bfloat16)
+
+    for j in range(2):
+        for k, start in enumerate((2 * j, 2 * j + 1, 4 + j, 6 + j)):
+            wsrc_ref[j, :, k * HEAD : (k + 1) * HEAD] = scaled(start * HEAD)
+        wsrc_ref[j, :, SLICE:] = proj_ref[:, 2 * HEAD * j : 2 * HEAD * (j + 1)]
+    ids_ref[:, :BLOCK] = jnp.broadcast_to(token_ref[...], (8, BLOCK))
+    ids_ref[:, BLOCK:] = jnp.zeros((8, HEAD - BLOCK), jnp.int32)
+
     def x_copy(j):
         return remote(
             wsrc_ref.at[j], w.at[x, seq], x_send.at[j], x_recv.at[x], seq, 2 * c + j, comm
         )
+
+    with jax.named_scope("barrier"):
+        @pl.when(is_comm)
+        def _():
+            pl.semaphore_wait(barrier, 54)
+
+        @pl.when(is_chain & jnp.logical_not(self_emb))
+        def _():
+            pl.semaphore_wait(barrier, 70)
+
+        @pl.when(self_emb)
+        def _():
+            pl.semaphore_wait(barrier, 68)
 
     for j in range(2):
         stays = is_comm & (x == j)
@@ -71,11 +134,6 @@
         @pl.when(stays)
         def _():
             w[x, seq] = wsrc_ref[j]
-
-    @pl.loop(0, tab.shape[0])
-    def _(k):
-        columns = pl.ds(pl.multiple_of(k * HEAD, HEAD), HEAD)
-        pltpu.make_async_copy(table_ref.at[:, columns], tab.at[k], tab_sem).start()
 
     def ids_copy(d):
         return remote(
@@ -103,74 +161,18 @@
 
     def y_copy(layer, way, step, zi, s):
         to = (seq + (NZ if way == 0 else SEQ - NZ)) % SEQ
+        if step == 3:
+            return remote(
+                w.at[layer, s], w.at[layer, s], y_send.at[layer, way], push_recv.at[layer],
+                to, x, chain,
+            )
         return remote(
             w.at[layer, s], w.at[layer, s], y_send.at[layer, way], y_recv.at[layer, way, step, zi],
             to, x, comm,
         )
 
-    @pl.when(is_comm)
-    def _():
-        for layer in range(LAYERS):
-            local = (x == layer) & (x < 2)
-
-            @pl.when(jnp.logical_not(local))
-            def _():
-                remote(
-                    w.at[layer, seq], w.at[layer, seq], x_send.at[0], x_recv.at[layer], seq, x, comm
-                ).wait_recv()
-
-            for dz in (1, 3, 2):
-                z_copy(layer, dz).start()
-            if layer == 0:
-                for way in range(2):
-                    y_copy(0, way, 0, 0, seq).start()
-            push(layer, seq)
-
-    @pl.loop(0, NY)
-    def _(b):
-        @pl.when(jnp.logical_not((zh == x) & (b == y)))
-        def _():
-            remote(
-                ids_ref, ids_v.at[b], ids_send.at[0], ids_recv.at[b], seq, x, tp
-            ).wait_recv()
-
-    to_scalar = pltpu.make_async_copy(ids_v, ids_s, ids_local)
-    to_scalar.start()
-    to_scalar.wait()
-    pltpu.make_async_copy(tab, tab, tab_sem).wait()
-    emb_section = 2 * c + seq // 16
-    lane = lax.broadcasted_iota(jnp.int32, (32, HEAD), 1)
-
-    def emb_copy(b):
-        return remote(
-            emb_out.at[b], emb_in.at[seq % 16], emb_send.at[b], emb_recv.at[seq % 16],
-            NZ * b + x, emb_section, chain,
-        )
-
-    def emb_self(b):
-        return is_chain & (emb_section == x) & (NZ * b + x == seq)
-
-    @pl.loop(0, NY)
-    def _(b):
-        def token(i, got):
-            v = ids_s[b, 0, i]
-            tile = tab[v >> 7].astype(jnp.float32)
-            column = jnp.sum(jnp.where(lane == (v & 127), tile, 0.0), axis=1, keepdims=True)
-            return jnp.where(lane == i, column, got)
-
-        got = lax.fori_loop(0, BLOCK, token, jnp.zeros((32, HEAD), jnp.float32), unroll=8)
-        emb_out[b] = got.astype(jnp.bfloat16)
-
-        @pl.when(jnp.logical_not(emb_self(b)))
-        def _():
-            emb_copy(b).start()
-
-        @pl.when(emb_self(b))
-        def _():
-            emb_in[seq % 16] = got.astype(jnp.bfloat16)
-
-    def own_sends(layer, first):
-        for zi in range(first, NZ):
+    def own_sends(layer):
+        for zi in range(NZ):
             dz = Z_STEPS[zi]
             s = NZ * y + (zh + NZ - dz) % NZ
             if zi > 0:
@@ -180,8 +182,80 @@
                 ).wait_recv()
             for way in range(2):
                 y_copy(layer, way, 0, zi, s).start()
-            if zi > 0:
-                push(layer, s)
+            push(layer, s)
+
+    def x_arrived(layer):
+        local = (x == layer) & (x < 2)
+
+        with jax.named_scope("x_wait"):
+            @pl.when(jnp.logical_not(local))
+            def _():
+                remote(
+                    w.at[layer, seq], w.at[layer, seq], x_send.at[0], x_recv.at[layer], seq, x, comm
+                ).wait_recv()
+
+    @pl.when(is_comm)
+    def _():
+        x_arrived(0)
+        for dz in (1, 3, 2):
+            z_copy(0, dz).start()
+        with jax.named_scope("own_first"):
+            own_sends(0)
+        for layer in range(1, LAYERS):
+            x_arrived(layer)
+
+    with jax.named_scope("ids_wait"):
+        @pl.loop(0, NY)
+        def _(b):
+            @pl.when(jnp.logical_not((zh == x) & (b == y)))
+            def _():
+                remote(
+                    ids_ref, ids_v.at[b], ids_send.at[0], ids_recv.at[b], seq, x, tp
+                ).wait_recv()
+
+    with jax.named_scope("table_wait"):
+        to_scalar = pltpu.make_async_copy(ids_v, ids_s, ids_local)
+        to_scalar.start()
+        to_scalar.wait()
+        table_copy.wait()
+    lane = lax.broadcasted_iota(jnp.int32, (32, HEAD), 1)
+    ones = jnp.ones((HEAD, HEAD), jnp.bfloat16)
+
+    def emb_copy(b):
+        return remote(
+            emb_out.at[b], emb_in.at[seq % 16], emb_send.at[b], emb_recv.at[seq % 16],
+            NZ * b + x, emb_section, chain,
+        )
+
+    def emb_self(b):
+        return self_emb & (b == y)
+
+    with jax.named_scope("gather"):
+        @pl.loop(0, NY)
+        def _(b):
+            def tokens(i, got):
+                picked = []
+                for k in range(8):
+                    v = ids_s[b, 0, 8 * i + k]
+                    tile = tab[:, v >> 7].reshape(32, HEAD)
+                    picked.append(jnp.where(lane == (v & 127), tile, jnp.zeros_like(tile)))
+                spread = jnp.dot(
+                    jnp.concatenate(picked, axis=0), ones, preferred_element_type=jnp.float32
+                )
+                for k in range(8):
+                    got = jnp.where(lane == 8 * i + k, spread[32 * k : 32 * (k + 1)], got)
+                return got
+
+            got = lax.fori_loop(0, 8, tokens, jnp.zeros((32, HEAD), jnp.float32))
+            emb_out[b] = got.astype(jnp.bfloat16)
+
+            @pl.when(jnp.logical_not(emb_self(b)))
+            def _():
+                emb_copy(b).start()
+
+            @pl.when(emb_self(b))
+            def _():
+                emb_in[seq % 16] = got.astype(jnp.bfloat16)
 
     def received(way, step, zi):
         row = (y + (NY - step if way == 0 else step)) % NY
@@ -194,24 +268,26 @@
 
     @pl.when(is_comm)
     def _():
-        own_sends(0, 1)
-
         @pl.loop(0, LAYERS)
         def _(layer):
-            for step in range(1, 4):
-                for zi in range(NZ):
-                    for way in range(2):
-                        s = arrived(layer, way, step, zi)
-                        if step < 3 or (zi < 2) == (way == 0):
-                            y_copy(layer, way, step, zi, s).start()
-                        push(layer, s)
-
             @pl.when(layer < LAYERS - 1)
             def _():
-                own_sends(layer + 1, 0)
-
-            for zi in range(NZ):
-                push(layer, arrived(layer, 0 if zi < 2 else 1, 4, zi))
+                for dz in (1, 3, 2):
+                    z_copy(layer + 1, dz).start()
+
+            with jax.named_scope("ring"):
+                for step in range(1, 4):
+                    for zi in range(NZ):
+                        for way in range(2):
+                            s = arrived(layer, way, step, zi)
+                            if step < 3 or (zi < 2) == (way == 0):
+                                y_copy(layer, way, step, zi, s).start()
+                            push(layer, s)
+
+            with jax.named_scope("own_next"):
+                @pl.when(layer < LAYERS - 1)
+                def _():
+                    own_sends(layer + 1)
 
         @pl.loop(0, LAYERS)
         def _(layer):
@@ -225,7 +301,8 @@
                 z_recv.at[layer, 1], seq, x, comm,
             ).wait_send()
             remote(
-                w.at[layer], w.at[layer], push_send.at[layer], push_recv.at[layer], seq, x, chain
+                w.at[layer, pl.ds(0, 28)], w.at[layer, pl.ds(0, 28)], push_send.at[layer],
+                push_recv.at[layer], seq, x, chain,
             ).wait_send()
 
     def member(d):
@@ -260,15 +337,14 @@
 
     @pl.when(is_chain)
     def _():
-        self_emb = (zh == x) & (x >= 2) & (seq // 16 == x % 2)
-
-        @pl.loop(0, 16)
-        def _(k):
-            @pl.when(jnp.logical_not(self_emb & (k == seq % 16)))
-            def _():
-                remote(
-                    emb_out.at[0], emb_in.at[k], emb_send.at[0], emb_recv.at[k], seq, x, tp
-                ).wait_recv()
+        with jax.named_scope("emb_wait"):
+            @pl.loop(0, 16)
+            def _(k):
+                @pl.when(jnp.logical_not(self_emb & (k == seq % 16)))
+                def _():
+                    remote(
+                        emb_out.at[0], emb_in.at[k], emb_send.at[0], emb_recv.at[k], seq, x, tp
+                    ).wait_recv()
 
         start = emb_in[...].reshape(SLICE, HEAD).astype(jnp.float32).T[:BLOCK]
         res[...] = start
@@ -293,9 +369,10 @@
 
         @pl.loop(0, LAYERS)
         def _(layer):
-            remote(
-                w.at[layer], w.at[layer], push_send.at[layer], push_recv.at[layer], seq, x, chain
-            ).wait_recv()
+            with jax.named_scope("w_wait"):
+                remote(
+                    w.at[layer], w.at[layer], push_send.at[layer], push_recv.at[layer], seq, x, chain
+                ).wait_recv()
 
             def add(d, square):
                 other = m ^ d
@@ -322,7 +399,8 @@
                 hf = h.astype(jnp.float32)
                 return square + jnp.sum(hf * hf, axis=1, keepdims=True)
 
-            square = lax.fori_loop(0, GROUP, add, jnp.zeros((BLOCK, 1), jnp.float32))
+            with jax.named_scope("ag_qkv"):
+                square = lax.fori_loop(0, GROUP, add, jnp.zeros((BLOCK, 1), jnp.float32))
             projected = acc[...] * lax.rsqrt(square * (1.0 / (GROUP * SLICE)) + EPS)
             q0 = rotated(projected[:, :HEAD])
             q1 = rotated(projected[:, HEAD : 2 * HEAD])
@@ -340,14 +418,15 @@
                 akv[layer, :, :HEAD] = key
                 akv[layer, :, HEAD:] = value
 
-            @pl.when(seq > 0)
-            def _():
-                kv_copy(layer, kv.at[layer], 0, seq).wait_recv()
-
-                @pl.when(zh == 0)
+            with jax.named_scope("kv_wait"):
+                @pl.when(seq > 0)
                 def _():
-                    for i in range(1, NZ):
-                        kv_copy(layer, akv.at[layer], NY + i, seq + i).start()
+                    kv_copy(layer, kv.at[layer], 0, seq).wait_recv()
+
+                    @pl.when(zh == 0)
+                    def _():
+                        for i in range(1, NZ):
+                            kv_copy(layer, akv.at[layer], NY + i, seq + i).start()
 
             queries = jnp.concatenate([q0, q1], axis=0)
             keys = jnp.concatenate([akv[layer, :, :HEAD], key], axis=0)
@@ -367,22 +446,24 @@
                     attended, weights, (((1,), (1,)), ((), ())), preferred_element_type=jnp.float32
                 )
 
-            @pl.loop(1, GROUP)
-            def _(d):
-                other = m ^ d
-                part_out[layer, other] = partial(other).astype(jnp.bfloat16)
-                rs_copy(layer, d).start()
-
-            acc[...] = partial(m)
-
-            @pl.loop(1, GROUP)
-            def _(d):
-                other = m ^ d
-                remote(
-                    part_out.at[layer, other], part_in.at[layer, other], rs_send.at[layer],
-                    rs_recv.at[layer, other], seq, x, chain,
-                ).wait_recv()
-                acc[...] += part_in[layer, other].astype(jnp.float32)
+            with jax.named_scope("partials"):
+                @pl.loop(1, GROUP)
+                def _(d):
+                    other = m ^ d
+                    part_out[layer, other] = partial(other).astype(jnp.bfloat16)
+                    rs_copy(layer, d).start()
+
+                acc[...] = partial(m)
+
+            with jax.named_scope("rs_wait"):
+                @pl.loop(1, GROUP)
+                def _(d):
+                    other = m ^ d
+                    remote(
+                        part_out.at[layer, other], part_in.at[layer, other], rs_send.at[layer],
+                        rs_recv.at[layer, other], seq, x, chain,
+                    ).wait_recv()
+                    acc[...] += part_in[layer, other].astype(jnp.float32)
 
             new = (res[...] + acc[...]).astype(jnp.bfloat16)
             res[...] = new.astype(jnp.float32)
@@ -463,24 +544,8 @@
 
 
 def body(token_ids, embed_columns, norm_gain, qkv_weight, out_weight):
-    seq = lax.axis_index("seq")
-    ids = jnp.broadcast_to(jnp.pad(token_ids, (0, HEAD - BLOCK))[None], (8, HEAD))
-    gain = lax.dynamic_slice_in_dim(norm_gain[0], seq * ROWS, ROWS, 0).astype(jnp.float32)
-    qkv = (qkv_weight[0].astype(jnp.float32) * gain[:, None]).astype(jnp.bfloat16)
-    out = out_weight[0]
-    pieces = [
-        jnp.concatenate(
-            [
-                qkv[:, 2 * HEAD * j : 2 * HEAD * (j + 1)],
-                qkv[:, HEAD * (4 + j) : HEAD * (5 + j)],
-                qkv[:, HEAD * (6 + j) : HEAD * (7 + j)],
-                out[:, 2 * HEAD * j : 2 * HEAD * (j + 1)],
-            ],
-            axis=1,
-        )
-        for j in range(2)
-    ]
-    sources = jnp.stack(pieces)
+    features, vocabulary = embed_columns.shape
+    table = embed_columns.reshape(features // 8, 8, vocabulary // HEAD, HEAD).transpose(0, 2, 1, 3)
     rope_a, rope_b = rope_constants()
     bf16, f32 = jnp.bfloat16, jnp.float32
     vmem = pl.BlockSpec(memory_space=pltpu.VMEM)
@@ -488,11 +553,13 @@
     states = pl.pallas_call(
         kernel,
         out_shape=jax.ShapeDtypeStruct((BLOCK, 2 * SLICE), bf16),
-        in_specs=[vmem, pl.BlockSpec(memory_space=pl.ANY), vmem, vmem, vmem],
+        in_specs=[vmem, pl.BlockSpec(memory_space=pl.ANY), vmem, vmem, vmem, vmem, vmem],
         out_specs=vmem,
         scratch_shapes=[
+            pltpu.VMEM((8, HEAD), jnp.int32),
+            pltpu.VMEM((2, ROWS, WIDE), bf16),
             pltpu.VMEM((LAYERS, SEQ, ROWS, WIDE), bf16),
-            pltpu.VMEM((embed_columns.shape[1] // HEAD, 32, HEAD), bf16),
+            pltpu.VMEM(table.shape, bf16),
             pltpu.VMEM((NY, 8, HEAD), jnp.int32),
             pltpu.SMEM((NY, 8, HEAD), jnp.int32),
             pltpu.VMEM((NY, 32, HEAD), bf16),
@@ -509,7 +576,7 @@
             dma((LAYERS,)),
             dma((LAYERS, NZ)),
             dma((LAYERS, 2)),
-            dma((LAYERS, 2, 4, NZ)),
+            dma((LAYERS, 2, 3, NZ)),
             dma((LAYERS,)),
             dma((LAYERS,)),
             dma((SEQ,)),
@@ -528,9 +595,12 @@
             dma((2,)),
         ],
         compiler_params=pltpu.CompilerParams(
-            has_side_effects=True, vmem_limit_bytes=62 * 1024 * 1024
+            collective_id=0, has_side_effects=True, vmem_limit_bytes=62 * 1024 * 1024
         ),
-    )(ids, embed_columns, sources, jnp.asarray(rope_a), jnp.asarray(rope_b))
+    )(
+        token_ids[None], table, norm_gain, qkv_weight[0], out_weight[0],
+        jnp.asarray(rope_a), jnp.asarray(rope_b),
+    )
     return states[None]
 
 

time: 199 us -> 183 us (0.920)
  Pallas kernels: 190 us -> 179 us
  other arithmetic: 2.54 us -> 0 us
  local copies, waits for them, and re-layouts: 3.74 us -> 1.57 us
    pallas_call x1, Pallas kernels: 190 us -> 179 us  [body(): pl.pallas_call(kernel, out_shape=jax.ShapeDtypeStruct((BLOCK, 2 * SLICE),...]
where the time goes in v2:
time: 183 us; the launch traced here: 181 us
  Pallas kernels  179 us (98%)
    pallas_call x1, Pallas kernels, body(): pl.pallas_call(kernel, out_shape=jax.ShapeDtypeStruct((BLOCK, 2 * SLICE),...  179 us

profile of v2, /device:TPU:1, one launch (start us, length us, event | category | flops | bytes accessed | tf_op | source)
XLA Modules:
  0.0 180.9 jit_solution(18089059822771808791)
XLA Ops:
  0.0 179.3 %shard_map.73 = bf16[64,1024]{1,0:T(8,128)(2,1)} custom-call(s32[1,64]{1,0:T(1,128)} %bitcast.11, bf16[4,512,8,128]{3,2,1,0:T(8,128)(2,1)} %bitcast.7, bf16[1,4096]{1,0:T(2,128)(2,1)} %gain_ref.1, bf16[128,1024]{1,0:T(8,128)(2,1)} %bitcast.9, bf16[128,512]{1,0:T(8,128)(2,1)} %bitcast.10, f32[32,256]{1,0:T(8,128)} %constant.4.clone.rope_a_ref, ...), custom_call_target="tpu_custom_call" | custom-call | tf_op jit(solution)/shard_map/pallas_call | solution.py:553
  179.4 1.6 copy.9
